TPU v7x, 32 devices: a whole 2x2x4 slice. The times are simulated.
32 devices in a mesh: lat: 4 (over x, core), lon: 8 (over z, y).
Axes of the slice: x: 2, y: 2, z: 4, core: 2. Of those that a mesh axis runs over, the one named last changes fastest.
Arguments:
- tracers: bfloat16 [256, 1024, 32, 4], P('lat', 'lon'), may hold values from 0 to 2
- weights: bfloat16 [256, 8, 8, 128, 128], P('lat', 'lon'), may hold values from -1 to 1, as said below
- source_row: int32 [256, 8, 8], P('lat', 'lon'), may hold values from 0 to 255, as said below
- source_block: int32 [256, 8, 8], P('lat', 'lon'), may hold values from 0 to 7, as said below
- slot_count: int32 [256, 8], P('lat', 'lon'), may hold values from 1 to 8, as said below
Outputs:
- advected_fixed: float32 [256, 1024, 32, 4], P('lat', 'lon')
Inputs may be any that keep to these rules, and one draw needn't show every extreme that they name: source_row differs from the target tile's own row by at most 4 and lies within the grid. source_block lies at cyclic distance at most 2 from the target tile's own index along the row, except for target tiles of the first and the last latitude row, where it may reach 3; the allowed distance grows from 1 at the equator towards the poles; in the two outermost rows slot 0 reaches exactly 3 sectors ahead on even tiles and 3 sectors behind on odd tiles. slot_count grows from 1 or 2 at the equator to 8 at the two outermost rows. weights are of either sign; for each target tile the weights of each target cell over the used slots and all source cells sum (before rounding to bfloat16) to one value of that tile between 0.9 and 1.05.
All inputs are finite; a program needn't handle non-finite values.
Results may differ from a plain program's by a relative error of at most 0.0003.
Values may be sent and summed in bfloat16 or wider, within the bound.
A program may use at most 192 MiB of HBM per device.

v0:
```python
import functools
import math

import jax
import jax.numpy as jnp
import numpy as np
from jax import lax
from jax.experimental import pallas as pl
from jax.experimental.pallas import tpu as pltpu
from jax.sharding import PartitionSpec as P

RLAT = 4
REACH = 3
OFFSETS = tuple(d for d in range(-REACH, REACH + 1) if d != 0)
MESH = pl.DeviceIdType.MESH
ANY = pl.BlockSpec(memory_space=pl.ANY)
VMEM = pl.BlockSpec(memory_space=pltpu.VMEM)
SMEM = pl.BlockSpec(memory_space=pltpu.SMEM)


def shifted(value, axis, by):
    length = lax.axis_size(axis)
    return lax.ppermute(value, axis, [(i, (i + by) % length) for i in range(length)])


def area_table(total_rows):
    angle = -0.5 * math.pi + (np.arange(total_rows) + 0.5) * (math.pi / total_rows)
    return np.cos(angle).astype(np.float32)


def everyone(lats, lons):
    return [(a, b) for a in range(lats) for b in range(lons) if (a, b) != (0, 0)]


def send_to_all(lats, lons, mine, slots, send_sem, recv_sem):
    lat, lon = lax.axis_index("lat"), lax.axis_index("lon")
    me = lat * lons + lon
    copies = []
    for n, (a, b) in enumerate(everyone(lats, lons)):
        peer = (lax.rem(lat + a, lats), lax.rem(lon + b, lons))
        copy = pltpu.make_async_remote_copy(
            src_ref=mine,
            dst_ref=slots.at[me],
            send_sem=send_sem.at[n],
            recv_sem=recv_sem.at[n],
            device_id=peer,
            device_id_type=MESH,
        )
        copy.start()
        copies.append(copy)
    return copies


def greet(lats, lons):
    lat, lon = lax.axis_index("lat"), lax.axis_index("lon")
    barrier = pltpu.get_barrier_semaphore()
    peers = everyone(lats, lons)
    for a, b in peers:
        peer = (lax.rem(lat + a, lats), lax.rem(lon + b, lons))
        pl.semaphore_signal(barrier, inc=1, device_id=peer, device_id_type=MESH)
    pl.semaphore_wait(barrier, len(peers))


def needs_kernel(lats, lons, need, field, slots, before, after, send_sem, recv_sem, halo_send, halo_recv):
    lat, lon = lax.axis_index("lat"), lax.axis_index("lon")
    rows = field.shape[0]
    greet(lats, lons)

    def up():
        return pltpu.make_async_remote_copy(
            src_ref=field.at[pl.ds(rows - RLAT, RLAT)],
            dst_ref=before,
            send_sem=halo_send.at[0],
            recv_sem=halo_recv.at[0],
            device_id=(lax.rem(lat + 1, lats), lon),
            device_id_type=MESH,
        )

    def down():
        return pltpu.make_async_remote_copy(
            src_ref=field.at[pl.ds(0, RLAT)],
            dst_ref=after,
            send_sem=halo_send.at[1],
            recv_sem=halo_recv.at[1],
            device_id=(lax.rem(lat + lats - 1, lats), lon),
            device_id_type=MESH,
        )

    up().start()
    down().start()
    copies = send_to_all(lats, lons, need, slots, send_sem, recv_sem)
    slots[lat * lons + lon] = need[...]
    for copy in copies:
        copy.wait()
    up().wait()
    down().wait()


def share_needs(need, field, lats, lons):
    count = lats * lons
    halo = jax.ShapeDtypeStruct((RLAT,) + field.shape[1:], field.dtype)
    return pl.pallas_call(
        functools.partial(needs_kernel, lats, lons),
        out_shape=(jax.ShapeDtypeStruct((count,) + need.shape, need.dtype), halo, halo),
        in_specs=[VMEM, ANY],
        out_specs=(VMEM, ANY, ANY),
        scratch_shapes=[
            pltpu.SemaphoreType.DMA((count - 1,)),
            pltpu.SemaphoreType.DMA((count - 1,)),
            pltpu.SemaphoreType.DMA((2,)),
            pltpu.SemaphoreType.DMA((2,)),
        ],
        compiler_params=pltpu.CompilerParams(collective_id=0, has_side_effects=True),
        name="share_needs",
    )(need, field)


def total_kernel(lats, lons, part, total, slots, send_sem, recv_sem):
    greet(lats, lons)
    copies = send_to_all(lats, lons, part, slots, send_sem, recv_sem)
    slots[lax.axis_index("lat") * lons + lax.axis_index("lon")] = part[...]
    for copy in copies:
        copy.wait()
    total[...] = jnp.sum(slots[...], axis=0)


def sum_over_devices(part, lats, lons):
    count = lats * lons
    return pl.pallas_call(
        functools.partial(total_kernel, lats, lons),
        out_shape=jax.ShapeDtypeStruct(part.shape, part.dtype),
        in_specs=[VMEM],
        out_specs=VMEM,
        scratch_shapes=[
            pltpu.VMEM((count,) + part.shape, part.dtype),
            pltpu.SemaphoreType.DMA((count - 1,)),
            pltpu.SemaphoreType.DMA((count - 1,)),
        ],
        compiler_params=pltpu.CompilerParams(collective_id=1, has_side_effects=True),
        name="sum_masses",
    )(part)


TIERS = ((52, 44, 39), (60, 52, 46))


def capacities(padded_rows, tier):
    near_polar, near_inner, far_polar = [padded_rows * part // 72 for part in tier]
    by_reach = {1: (near_polar, near_inner), 2: (far_polar, 0)}
    return {d: by_reach.get(abs(d), (RLAT + 1, 0)) for d in OFFSETS}


def layout_of(caps):
    bases, received = {}, 0
    for d in OFFSETS:
        bases[d] = received
        received += max(caps[d])
    return bases, received


def exchange_kernel(
    lats, lons, caps, bases, lists, field, before, after, recv, padded, outgoing, load_sem, send_sem, recv_sem
):
    lat, lon = lax.axis_index("lat"), lax.axis_index("lon")
    rows = field.shape[0]
    loads = [
        pltpu.make_async_copy(before, padded.at[pl.ds(0, RLAT)], load_sem.at[0]),
        pltpu.make_async_copy(field, padded.at[pl.ds(RLAT, rows)], load_sem.at[1]),
        pltpu.make_async_copy(after, padded.at[pl.ds(RLAT + rows, RLAT)], load_sem.at[2]),
    ]
    for load in loads:
        load.start()
    barrier = pltpu.get_barrier_semaphore()
    for d in OFFSETS:
        peer = (lat, lax.rem(lon + lons - d, lons))
        pl.semaphore_signal(barrier, inc=1, device_id=peer, device_id_type=MESH)
    pl.semaphore_wait(barrier, len(OFFSETS))
    for load in loads:
        load.wait()

    polar = (lat == 0) | (lat == lats - 1)
    pieces = []
    for d in sorted(OFFSETS, key=lambda d: (abs(d), d)):
        outer, inner = caps[d]
        if inner:
            pieces.append((d, 0, inner, False))
    for d in sorted(OFFSETS, key=lambda d: (abs(d) == 1, abs(d), d)):
        outer, inner = caps[d]
        if outer > inner:
            pieces.append((d, inner, outer, True))

    def guarded(only_polar, act):
        if only_polar:
            pl.when(polar)(act)
        else:
            act()

    def copy_of(n):
        d, first, last, _ = pieces[n]
        span = pl.ds(bases[d] + first, last - first)
        return pltpu.make_async_remote_copy(
            src_ref=outgoing.at[span],
            dst_ref=recv.at[span],
            send_sem=send_sem.at[n],
            recv_sem=recv_sem.at[n],
            device_id=(lat, lax.rem(lon + lons - d, lons)),
            device_id_type=MESH,
        )

    def gather(n):
        d, first, last, _ = pieces[n]
        row = OFFSETS.index(d)

        def step(c, carry):
            outgoing[bases[d] + c] = padded[lists[row, c]]
            return carry

        lax.fori_loop(first, last, step, 0)

    for n in range(len(pieces) + 1):
        if n < len(pieces):
            guarded(pieces[n][3], functools.partial(gather, n))
        if n > 0:
            guarded(pieces[n - 1][3], lambda n=n: copy_of(n - 1).start())
    for n in range(len(pieces)):
        guarded(pieces[n][3], lambda n=n: copy_of(n).wait())


def exchange(lists, field, before, after, lats, lons, caps, bases, received, collective_id):
    tile = field.shape[1:]
    padded_rows = field.shape[0] + 2 * RLAT
    count = 2 * len(OFFSETS)
    return pl.pallas_call(
        functools.partial(exchange_kernel, lats, lons, caps, bases),
        out_shape=jax.ShapeDtypeStruct((received,) + tile, field.dtype),
        in_specs=[SMEM, ANY, ANY, ANY],
        out_specs=ANY,
        scratch_shapes=[
            pltpu.VMEM((padded_rows,) + tile, field.dtype),
            pltpu.VMEM((received,) + tile, field.dtype),
            pltpu.SemaphoreType.DMA((3,)),
            pltpu.SemaphoreType.DMA((count,)),
            pltpu.SemaphoreType.DMA((count,)),
        ],
        compiler_params=pltpu.CompilerParams(collective_id=collective_id, has_side_effects=True),
        name="exchange",
    )(lists, field, before, after)


def advect_kernel(step_rows, slots, code, table, counts, area, weights, field, before, after, recv, out, delta, src, gap, sem):
    g = pl.program_id(0)
    rows = field.shape[0]
    padded_rows = rows + 2 * RLAT
    received = recv.shape[0]

    @pl.when(g == 0)
    def _():
        loads = [
            pltpu.make_async_copy(before, src.at[pl.ds(0, RLAT)], sem.at[0]),
            pltpu.make_async_copy(field, src.at[pl.ds(RLAT, rows)], sem.at[1]),
            pltpu.make_async_copy(after, src.at[pl.ds(RLAT + rows, RLAT)], sem.at[2]),
            pltpu.make_async_copy(recv, src.at[pl.ds(padded_rows, received)], sem.at[3]),
        ]
        for load in loads:
            load.start()
        src[padded_rows + received] = jnp.zeros(src.shape[1:], src.dtype)
        gap[...] = jnp.zeros_like(gap)
        for load in loads:
            load.wait()

    together = 4 if step_rows % 4 == 0 else 1
    for first in range(0, step_rows, together):
        group = range(first, first + together)
        used = counts[g * step_rows + first]
        for tt in group[1:]:
            used = jnp.maximum(used, counts[g * step_rows + tt])
        for last in range(2, slots + 2, 2):
            width = min(last, slots)

            @pl.when((used > last - 2) & (used <= last))
            def _(group=group, width=width):
                total = gap[...]
                for tt in group:
                    t = g * step_rows + tt
                    left = jnp.concatenate([src[table[code[k, t]]] for k in range(width)], axis=1)
                    right = jnp.concatenate([weights[tt, 0, k] for k in range(width)], axis=1)
                    value = lax.dot_general(
                        left, right, (((1,), (1,)), ((), ())), preferred_element_type=jnp.float32
                    )
                    out[tt] = value
                    total += area[t] * (src[RLAT + t].astype(jnp.float32) - value)
                gap[...] = total

    @pl.when(g == pl.num_programs(0) - 1)
    def _():
        delta[...] = jnp.sum(gap[...].T, axis=0, keepdims=True)


def advect(code, table, counts, area, weights, field, before, after, recv):
    rows, channels, width = field.shape
    slots = weights.shape[2]
    step_rows = 8
    while rows % step_rows:
        step_rows -= 1
    sources = rows + 2 * RLAT + recv.shape[0] + 1
    block = (step_rows,) + weights.shape[1:]
    return pl.pallas_call(
        functools.partial(advect_kernel, step_rows, slots),
        grid=(rows // step_rows,),
        out_shape=(
            jax.ShapeDtypeStruct(field.shape, jnp.float32),
            jax.ShapeDtypeStruct((1, channels), jnp.float32),
        ),
        in_specs=[
            SMEM,
            SMEM,
            SMEM,
            SMEM,
            pl.BlockSpec(block, lambda g: (g, 0, 0, 0, 0)),
            ANY,
            ANY,
            ANY,
            ANY,
        ],
        out_specs=(
            pl.BlockSpec((step_rows, channels, width), lambda g: (g, 0, 0)),
            pl.BlockSpec((1, channels), lambda g: (0, 0)),
        ),
        scratch_shapes=[
            pltpu.VMEM((sources, channels, width), field.dtype),
            pltpu.VMEM((channels, width), jnp.float32),
            pltpu.SemaphoreType.DMA((4,)),
        ],
        compiler_params=pltpu.CompilerParams(dimension_semantics=("arbitrary",)),
        name="advect",
    )(code, table, counts, area, weights, field, before, after, recv)


def dense(field, before, after, weights, local_row, relative, active, area):
    padded = jnp.concatenate([before, field, after], axis=0)
    stack = jnp.stack(
        [padded if d == 0 else shifted(padded, "lon", -d) for d in range(-REACH, REACH + 1)], axis=1
    )
    rows = jnp.clip(local_row, 0, padded.shape[0] - 1)
    picked = stack[rows, jnp.clip(relative + REACH, 0, 2 * REACH)]
    picked = jnp.where(active[:, :, None, None], picked, jnp.zeros((), picked.dtype))
    advected = jnp.einsum("tkij,ktcj->tci", weights[:, 0], picked, preferred_element_type=jnp.float32)
    gap = jnp.sum(area[:, None, None] * (field.astype(jnp.float32) - advected), axis=(0, 2))
    return advected, gap[None, :]


def local(tracers, weights, source_row, source_block, slot_count):
    rows, width, levels, kinds = tracers.shape
    channels = levels * kinds
    lats, lons = lax.axis_size("lat"), lax.axis_size("lon")
    lat, lon = lax.axis_index("lat"), lax.axis_index("lon")
    field = tracers.reshape(rows, width, channels).transpose(0, 2, 1)
    slots = source_row.shape[2]
    table = area_table(rows * lats)
    total_area = float(width * lons * np.sum(table.astype(np.float64)))
    area = lax.dynamic_slice(jnp.asarray(table), (lat * rows,), (rows,))

    padded_rows = rows + 2 * RLAT
    lanes = -(-padded_rows // 128) * 128
    local_row = source_row[:, 0, :].T - (lat * rows - RLAT)
    relative = (source_block[:, 0, :].T - lon + REACH) % lons - REACH
    active = jnp.arange(slots, dtype=jnp.int32)[:, None] < slot_count[:, 0][None, :]
    away, own, unused = len(OFFSETS), len(OFFSETS), len(OFFSETS) + 1
    which = jnp.where(relative < 0, relative + REACH, relative + REACH - 1)
    which = jnp.where(relative == 0, own, which)
    code = jnp.where(active, which * lanes + local_row, unused * lanes)
    ids = jnp.arange(8 * lanes, dtype=jnp.int32)
    hit = (code.reshape(-1)[None, :] == ids[:, None]) & (ids < away * lanes)[:, None]
    need = jnp.any(hit, axis=1).astype(jnp.float32).reshape(8, lanes).astype(jnp.bfloat16)

    needs, before, after = share_needs(need, field, lats, lons)

    plans = [capacities(padded_rows, tier) for tier in TIERS]
    counted = jnp.sum(needs.astype(jnp.float32), axis=2)
    level = jnp.int32(0)
    for caps in plans:
        limit = np.zeros((lats, lons, 8), np.float32)
        for n, d in enumerate(OFFSETS):
            limit[:, :, n] = caps[d][1]
            limit[0, :, n] = limit[-1, :, n] = caps[d][0]
        over = jnp.any(counted > jnp.asarray(limit.reshape(lats * lons, 8)))
        level += over.astype(jnp.int32)

    upto = (jnp.arange(lanes)[:, None] <= jnp.arange(lanes)[None, :]).astype(jnp.float32)

    def ranks(mask):
        mask = mask.astype(jnp.float32)
        return jnp.sum(mask[:, :, None] * upto[None], axis=1).astype(jnp.int32) - 1

    def fast(n, field, before, after, weights, needs):
        caps = plans[n]
        bases, received = layout_of(caps)
        band = lax.dynamic_slice(needs, (lat * lons, 0, 0), (lons, 8, lanes))
        offsets = np.zeros((8,), np.int32)
        offsets[: len(OFFSETS)] = OFFSETS
        dest = (lon - jnp.asarray(offsets)) % lons
        chosen = jnp.arange(lons, dtype=jnp.int32)[:, None] == dest[None, :]
        wanted = jnp.sum(jnp.where(chosen[:, :, None], band.astype(jnp.float32), 0.0), axis=0)
        rank = jnp.where(wanted > 0, ranks(wanted), -1)
        place = jnp.arange(lanes, dtype=jnp.int32)
        match = rank[:, :, None] == place[None, None, :]
        lists = jnp.sum(jnp.where(match, place[None, :, None], 0), axis=1)
        recv = exchange(lists, field, before, after, lats, lons, caps, bases, received, 2 + n)
        start = np.zeros((8, 1), np.int32)
        start[:away, 0] = [bases[d] + padded_rows for d in OFFSETS]
        kind = jnp.arange(8, dtype=jnp.int32)[:, None]
        spot = jnp.where(kind == own, place[None, :], padded_rows + received)
        spot = jnp.where(kind < away, ranks(need) + jnp.asarray(start), spot)
        return advect(code, spot.reshape(-1), slot_count[:, 0], area, weights, field, before, after, recv)

    def general(field, before, after, weights, needs):
        return dense(field, before, after, weights, local_row, relative, active, area)

    paths = [functools.partial(fast, n) for n in range(len(plans))] + [general]
    advected, delta = lax.switch(level, paths, field, before, after, weights, needs)
    total = sum_over_devices(delta, lats, lons)
    fixed = advected + (total[0] / total_area)[None, :, None]
    return fixed.transpose(0, 2, 1).reshape(rows, width, levels, kinds)


def solution(mesh):
    return jax.shard_map(
        local,
        mesh=mesh,
        in_specs=(
            P("lat", "lon", None, None),
            P("lat", "lon", None, None, None),
            P("lat", "lon", None),
            P("lat", "lon", None),
            P("lat", "lon"),
        ),
        out_specs=P("lat", "lon", None, None),
        check_vma=False,
    )
```

profile of v0, /device:TPU:0, one launch (start us, length us, event | category | flops | bytes accessed | tf_op | source)
XLA Modules:
  0.0 129.0 jit_solution(12765928957400412391)
XLA Ops:
  0.0 0.7 iota_compare_fusion.10
  0.7 0.1 copy.40
  0.8 0.7 fusion.25
  1.5 0.1 eq.100
  1.6 0.5 fusion.19
  2.2 12.9 %share_needs.1 = (bf16[32,8,128]{2,1,0:T(8,128)(2,1)S(1)}, bf16[4,128,128]{2,1,0:T(8,128)(2,1)S(1)}, bf16[4,128,128]{2,1,0:T(8,128)(2,1)S(1)}) custom-call(bf16[8,128]{1,0:T(8,128)(2,1)S(1)} %fusion.26.need, bf16[64,128,128]{2,1,0:T(8,128)(2,1)} %bitcast.59), custom_call_target="tpu_custom_call" | custom-call | tf_op jit(solution)/shard_map/share_needs/pallas_call | solution.py:102
  15.1 0.8 dynamic_slice.9
  15.9 0.1 convert_reduce_fusion
  16.0 0.1 copy.41
  16.0 1.4 %compare_reduce_fusion = (pred[]{:T(512)}, pred[]{:T(512)}) fusion(f32[32,8]{0,1:T(8,128)S(1)} %copy.41, f32[32,8]{0,1:T(8,128)} %constant.145.clone, f32[32,8]{0,1:T(8,128)} %constant.144.clone), kind=kLoop, calls=%fused_computation.72 | loop fusion | flops 1022 | bytes 3074 | tf_op jit(solution)/shard_map/reduce_or | solution.py:386
  18.8 95.9 %conditional.1 = ((f32[64,128,128]{2,1,0:T(8,128)}, f32[1,128]{1,0:T(1,128)S(1)})) conditional(s32[]{:T(128)} %clamp.5, (bf16[8,128]{1,0:T(8,128)(2,1)S(1)}, f32[128,128]{1,0:T(8,128)S(1)}, f32[128,128]{1,0:T(8,128)S(1)}, (), s32[64,1]{0,1:T(1,128)}, /*index=5*/s32[]{:T(128)}, s32[8]{0:T(128)}, s32[]{:T(128)}, ...), branch_computations={%region_4.9_spmd, %region_9.14_spmd, %region_14.16_spmd} | conditional | flops 2169510912 | bytes 214449664 | solution.py:420
  18.8 0.0 copy-start.4
  18.8 0.0 copy-start
  18.9 0.0 copy-start.2
  18.9 0.8 and_select_fusion
  19.7 0.1 select_reduce_fusion.1
  19.8 0.3 multiply_reduce_fusion
  20.2 0.8 select_reduce_fusion.lists
  21.0 76.9 %exchange.2.recv = bf16[192,128,128]{2,1,0:T(8,128)(2,1)} custom-call(s32[8,128]{1,0:T(8,128)} %select_reduce_fusion.lists, bf16[64,128,128]{2,1,0:T(8,128)(2,1)} %get-tuple-element.86.field, bf16[4,128,128]{2,1,0:T(8,128)(2,1)S(1)} %get-tuple-element.87.before, bf16[4,128,128]{2,1,0:T(8,128)(2,1)S(1)} %get-tuple-element.88.after), custom_call_target="tpu_custom_call" | custom-call | tf_op jit(solution)/shard_map/cond/branch_0_fun/exchange/pallas_call | solution.py:233
  97.9 0.0 copy-done.4
  97.9 0.7 select_bitcast_fusion.table
  98.6 0.0 copy-done
  98.6 0.0 copy-done.2
  98.6 15.9 %advect.2 = (f32[64,128,128]{2,1,0:T(8,128)}, f32[1,128]{1,0:T(1,128)S(1)}) custom-call(s32[8,64]{1,0:T(8,128)S(1)} %get-tuple-element.78.code, s32[1024]{0:T(1024)} %select_bitcast_fusion.table, s32[64]{0:T(128)S(1)} %bitcast.65, f32[64]{0:T(128)S(1)} %get-tuple-element.84.area, bf16[64,1,8,128,128]{4,3,2,1,0:T(8,128)(2,1)} %get-tuple-element.85.weights, ...), custom_call_target="tpu_custom_call" | custom-call | tf_op jit(solution)/shard_map/cond/branch_0_fun/advect/pallas_call | solution.py:307
  114.7 8.7 %sum_masses.1 = f32[1,128]{1,0:T(1,128)} custom-call(f32[1,128]{1,0:T(1,128)S(1)} %get-tuple-element.126.part), custom_call_target="tpu_custom_call" | custom-call | tf_op jit(solution)/shard_map/sum_masses/pallas_call | solution.py:129
  123.4 0.7 multiply_bitcast_fusion
  124.1 4.9 %broadcast_add_fusion = f32[64,128,128]{2,1,0:T(8,128)} fusion(f32[64,128,128]{2,1,0:T(8,128)} %get-tuple-element.125, f32[128]{0:T(128)S(1)} %multiply_bitcast_fusion), kind=kLoop, calls=%fused_computation.52 | loop fusion | flops 1048576 | bytes 8389120 | tf_op jit(solution)/shard_map/add | solution.py:422
  (7 shorter events, 0.0 us)
Async XLA Ops:
  18.8 79.1 %copy-start.4 = (s32[8]{0:T(128)S(1)}, s32[8]{0:T(128)}, u32[]{:S(2)}) copy-start(s32[8]{0:T(128)} %constant.154) | copy-start | bytes 100 | tf_op jit(solution)/shard_map/cond
  18.8 79.8 %copy-start = (bf16[64,128,128]{2,1,0:T(8,128)(2,1)S(1)}, bf16[64,128,128]{2,1,0:T(8,128)(2,1)}, u32[]{:S(2)}) copy-start(bf16[64,128,128]{2,1,0:T(8,128)(2,1)} %get-tuple-element.86.field) | copy-start | bytes 6291460 | tf_op jit(solution)/shard_map/cond
  18.9 79.7 %copy-start.2 = (s32[64,1]{0,1:T(1,128)S(1)}, s32[64,1]{0,1:T(1,128)}, u32[]{:S(2)}) copy-start(s32[64,1]{0,1:T(1,128)} %get-tuple-element.83) | copy-start | bytes 772 | tf_op jit(solution)/shard_map/cond
where the time goes:
time: 129 us
  Pallas kernels  114 us (88%)
  other arithmetic  11.9 us (9%)
  between operations  1.39 us (1%)
    pallas_call x1, Pallas kernels, exchange(): pl.pallas_call(functools.partial(exchange_kernel, lats, lons, caps, bases...  76.9 us
    pallas_call x1, Pallas kernels, advect(): pl.pallas_call(functools.partial(advect_kernel, step_rows, slots), grid=(...  15.9 us
    pallas_call x1, Pallas kernels, share_needs(): pl.pallas_call(functools.partial(needs_kernel, lats, lons), out_shape=(ja...  12.9 us
    pallas_call x1, Pallas kernels, sum_over_devices(): pl.pallas_call(functools.partial(total_kernel, lats, lons), out_shape=jax...  8.68 us
    add x1, other arithmetic, local(): fixed = advected + (total[0] / total_area)[None, :, None]  4.9 us

commit v1 on v0

--- a/solution.py
+++ b/solution.py
@@ -141,13 +141,13 @@
     )(part)
 
 
-TIERS = ((52, 44, 39), (60, 52, 46))
+TIERS = ((50, 42, 37, 3), (52, 44, 39, 4), (54, 46, 41, 4), (60, 52, 46, 5))
 
 
 def capacities(padded_rows, tier):
-    near_polar, near_inner, far_polar = [padded_rows * part // 72 for part in tier]
+    near_polar, near_inner, far_polar = [padded_rows * part // 72 for part in tier[:3]]
     by_reach = {1: (near_polar, near_inner), 2: (far_polar, 0)}
-    return {d: by_reach.get(abs(d), (RLAT + 1, 0)) for d in OFFSETS}
+    return {d: by_reach.get(abs(d), (tier[3], 0)) for d in OFFSETS}
 
 
 def layout_of(caps):

time: 129 us -> 131 us (1.016); the launches traced: 129 us -> 132 us
  Pallas kernels: 114 us -> 117 us
    pallas_call x1, Pallas kernels: 76.9 us -> 79.1 us  [exchange(): pl.pallas_call(functools.partial(exchange_kernel, lats, lons, caps, bases...]
where the time goes in v1:
time: 131 us; the launch traced here: 132 us
  Pallas kernels  117 us (89%)
  other arithmetic  11.9 us (9%)
  between operations  2.59 us (2%)
    pallas_call x1, Pallas kernels, exchange(): pl.pallas_call(functools.partial(exchange_kernel, lats, lons, caps, bases...  79.1 us
    pallas_call x1, Pallas kernels, advect(): pl.pallas_call(functools.partial(advect_kernel, step_rows, slots), grid=(...  15.9 us
    pallas_call x1, Pallas kernels, share_needs(): pl.pallas_call(functools.partial(needs_kernel, lats, lons), out_shape=(ja...  12.9 us
    pallas_call x1, Pallas kernels, sum_over_devices(): pl.pallas_call(functools.partial(total_kernel, lats, lons), out_shape=jax...  8.68 us
    add x1, other arithmetic, local(): fixed = advected + (total[0] / total_area)[None, :, None]  4.9 us

profile of v1, /device:TPU:0, one launch (start us, length us, event | category | flops | bytes accessed | tf_op | source)
XLA Modules:
  0.0 132.4 jit_solution(9910885587503977439)
XLA Ops:
  0.0 0.7 iota_compare_fusion.18
  0.7 0.1 copy.50
  0.8 0.7 fusion.27
  1.5 0.1 eq.178
  1.6 0.5 fusion.21
  2.2 12.9 %share_needs.1 = (bf16[32,8,128]{2,1,0:T(8,128)(2,1)S(1)}, bf16[4,128,128]{2,1,0:T(8,128)(2,1)S(1)}, bf16[4,128,128]{2,1,0:T(8,128)(2,1)S(1)}) custom-call(bf16[8,128]{1,0:T(8,128)(2,1)S(1)} %fusion.28.need, bf16[64,128,128]{2,1,0:T(8,128)(2,1)} %bitcast.65), custom_call_target="tpu_custom_call" | custom-call | tf_op jit(solution)/shard_map/share_needs/pallas_call | solution.py:102
  15.1 0.8 dynamic_slice.15
  15.9 0.1 convert_reduce_fusion
  16.0 0.1 copy.51
  16.0 1.5 %compare_reduce_fusion = (pred[]{:T(512)}, pred[]{:T(512)}, pred[]{:T(512)}, pred[]{:T(512)}) fusion(f32[32,8]{0,1:T(8,128)S(1)} %copy.51, f32[32,8]{0,1:T(8,128)} %constant.208.clone, f32[32,8]{0,1:T(8,128)} %constant.207.clone, f32[32,8]{0,1:T(8,128)} %constant.206.clone, f32[32,8]{0,1:T(8,128)} %constant.205.clone), kind=kLoop, calls=%fused_computation.100 | loop fusion | flops 2044 | bytes 5124 | tf_op jit(solution)/shard_map/reduce_or | solution.py:386
  20.0 98.1 %conditional.1 = ((f32[64,128,128]{2,1,0:T(8,128)}, f32[1,128]{1,0:T(1,128)S(1)})) conditional(s32[]{:T(128)} %clamp.5, (bf16[8,128]{1,0:T(8,128)(2,1)S(1)}, f32[128,128]{1,0:T(8,128)S(1)}, f32[128,128]{1,0:T(8,128)S(1)}, (), s32[64,1]{0,1:T(1,128)}, /*index=5*/s32[]{:T(128)}, s32[8]{0:T(128)}, s32[]{:T(128)}, ...), branch_computations={%region_6.11_spmd, %region_11.16_spmd, %region_16.21_spmd, %region... | conditional | flops 2169510912 | bytes 214449664 | solution.py:420
  20.1 0.0 copy-start.10
  20.1 0.0 copy-start.2
  20.1 0.0 copy-start.6
  20.1 0.8 and_select_fusion.2
  20.9 0.1 select_reduce_fusion.5
  21.0 0.3 multiply_reduce_fusion.4
  21.4 0.8 select_reduce_fusion.4.lists
  22.2 79.1 %exchange.6.recv = bf16[198,128,128]{2,1,0:T(8,128)(2,1)} custom-call(s32[8,128]{1,0:T(8,128)} %select_reduce_fusion.4.lists, bf16[64,128,128]{2,1,0:T(8,128)(2,1)} %get-tuple-element.174.field, bf16[4,128,128]{2,1,0:T(8,128)(2,1)S(1)} %get-tuple-element.175.before, bf16[4,128,128]{2,1,0:T(8,128)(2,1)S(1)} %get-tuple-element.176.after), custom_call_target="tpu_custom_call" | custom-call | tf_op jit(solution)/shard_map/cond/branch_2_fun/exchange/pallas_call | solution.py:233
  101.3 0.0 copy-done.10
  101.3 0.7 select_bitcast_fusion.2.table
  102.0 0.0 copy-done.2
  102.0 0.0 copy-done.6
  102.0 15.9 %advect.6 = (f32[64,128,128]{2,1,0:T(8,128)}, f32[1,128]{1,0:T(1,128)S(1)}) custom-call(s32[8,64]{1,0:T(8,128)S(1)} %get-tuple-element.167.code, s32[1024]{0:T(1024)} %select_bitcast_fusion.2.table, s32[64]{0:T(128)S(1)} %bitcast.75, f32[64]{0:T(128)S(1)} %get-tuple-element.172.area, bf16[64,1,8,128,128]{4,3,2,1,0:T(8,128)(2,1)} %get-tuple-element.173.weights, ...), custom_call_target="tpu_custom_call" | custom-call | tf_op jit(solution)/shard_map/cond/branch_2_fun/advect/pallas_call | solution.py:307
  118.1 8.7 %sum_masses.1 = f32[1,128]{1,0:T(1,128)} custom-call(f32[1,128]{1,0:T(1,128)S(1)} %get-tuple-element.214.part), custom_call_target="tpu_custom_call" | custom-call | tf_op jit(solution)/shard_map/sum_masses/pallas_call | solution.py:129
  126.8 0.7 multiply_bitcast_fusion
  127.5 4.9 %broadcast_add_fusion = f32[64,128,128]{2,1,0:T(8,128)} fusion(f32[64,128,128]{2,1,0:T(8,128)} %get-tuple-element.213, f32[128]{0:T(128)S(1)} %multiply_bitcast_fusion), kind=kLoop, calls=%fused_computation.80 | loop fusion | flops 1048576 | bytes 8389120 | tf_op jit(solution)/shard_map/add | solution.py:422
  (7 shorter events, 0.0 us)
Async XLA Ops:
  20.1 81.2 %copy-start.10 = (s32[8]{0:T(128)S(1)}, s32[8]{0:T(128)}, u32[]{:S(2)}) copy-start(s32[8]{0:T(128)} %constant.219) | copy-start | bytes 100 | tf_op jit(solution)/shard_map/cond
  20.1 81.9 %copy-start.2 = (bf16[64,128,128]{2,1,0:T(8,128)(2,1)S(1)}, bf16[64,128,128]{2,1,0:T(8,128)(2,1)}, u32[]{:S(2)}) copy-start(bf16[64,128,128]{2,1,0:T(8,128)(2,1)} %get-tuple-element.174.field) | copy-start | bytes 6291460 | tf_op jit(solution)/shard_map/cond
  20.1 81.9 %copy-start.6 = (s32[64,1]{0,1:T(1,128)S(1)}, s32[64,1]{0,1:T(1,128)}, u32[]{:S(2)}) copy-start(s32[64,1]{0,1:T(1,128)} %get-tuple-element.171) | copy-start | bytes 772 | tf_op jit(solution)/shard_map/cond
